TPU v7x, 32 devices: a 4x4x1 block of a 4x4x8 slice. The times are simulated.
32 devices in a mesh: spin: 1 (over z), depth: 4 (over y), row: 4 (over x), col: 2 (over core).
Axes of the slice: x: 4, y: 4, z: 1, core: 2. Of those that a mesh axis runs over, the one named last changes fastest.
The devices are a block of a 4x4x8 slice.
Arguments:
- hamiltonian: float32 [6, 2048, 2048], P('spin', 'row', 'col')
- spec_bounds: float32 [6, 2], P('spin')
- occ_count: int32 [6], P('spin')
Outputs:
- output 1: float32 [6, 2048, 2048], P('spin', 'row', 'col')
- output 2: float32 [6], P('spin')
All inputs are finite; a program needn't handle non-finite values.
Results may differ from a plain program's by a relative error of at most 0.001.
Values sent between devices are 32-bit elements.
A program may use at most 768 MiB of HBM per device.

v0:
```python
import functools

import jax
import jax.numpy as jnp
from jax import lax
from jax.experimental import pallas as pl
from jax.experimental.pallas import tpu as pltpu
from jax.sharding import PartitionSpec as P

STEPS = 3
PIECES = 4
MESH = pl.DeviceIdType.MESH
F32 = jnp.float32
HIGHEST = lax.Precision.HIGHEST


def dot_nn(a, b):
    return jnp.dot(a, b, precision=HIGHEST, preferred_element_type=F32)


def dot_nt(a, b):
    return lax.dot_general(a, b, (((1,), (1,)), ((), ())), precision=HIGHEST, preferred_element_type=F32)


def kernel(
    sizes, ham, bounds, occ, out, energy_out, relay,
    hb, xb, ps, pr, ts, tr, es, er,
    in_send, in_recv_d, in_recv_o, tmp_send, tmp_recv,
    p_send, p_recv, t_send, t_recv,
    x_send, x_recv, r_send, r_recv, y_send, y_recv, e_send, e_recv, ey_send, ey_recv,
):
    slots, depth_size, row_size, col_size = sizes
    half = ham.shape[1]
    order = hb.shape[1]
    piece = half // PIECES
    up_pieces = tuple(range(PIECES // 2))
    down_pieces = tuple(range(PIECES // 2, PIECES))
    in_turn = tuple(k for pair in zip(up_pieces, down_pieces) for k in pair)
    full_order = order * col_size
    spin = lax.axis_index('spin')
    q = lax.axis_index('depth')
    r = lax.axis_index('row')
    c = lax.axis_index('col')
    par = lax.rem(q, 2)
    grp = r // 2
    q_up = lax.rem(q + 1, depth_size)
    q_dn = lax.rem(q + depth_size - 1, depth_size)

    def dev(qq, rr, cc):
        return (spin, qq, rr, cc)

    def rcopy(src, dst, ssem, rsem, target):
        return pltpu.make_async_remote_copy(
            src_ref=src, dst_ref=dst, send_sem=ssem, recv_sem=rsem, device_id=target, device_id_type=MESH
        )

    def wait_for(dst, sem):
        pltpu.make_async_copy(dst, dst, sem).wait()

    def aligned(start, size):
        return pl.ds(pl.multiple_of(start, size), size)

    barrier = pltpu.get_barrier_semaphore()
    for dr in range(row_size):
        for dc in range(col_size):
            if dr or dc:
                target = dev(q, lax.rem(r + dr, row_size), lax.rem(c + dc, col_size))
                pl.semaphore_signal(barrier, inc=1, device_id=target, device_id_type=MESH)
    for qq in (q_up, q_dn):
        pl.semaphore_signal(barrier, inc=1, device_id=dev(qq, r, c), device_id_type=MESH)
    pl.semaphore_wait(barrier, row_size * col_size + 1)

    def slot_of(x):
        return jnp.where(x < slots, x, x - 2)

    def alone(x):
        return lax.rem(x, 2) == 0

    def in_parts(s):
        g = s // 2
        mat = par * slots + slot_of(s)
        full_half = ham.at[mat]
        diag_cols = aligned(lax.rem(r, 2) * half, half)
        rows = aligned(lax.rem(r, 2) * half, half)
        in_g = grp == g
        d_sender = c == grp
        own_d = jnp.logical_and(d_sender, r == s)
        far_full = jnp.logical_and(d_sender, jnp.logical_and(jnp.logical_not(in_g), lax.rem(r, 2) == 1 - s % 2))
        near_diag = jnp.logical_and(in_g, r != s)
        far_diag = jnp.logical_and(jnp.logical_not(in_g), lax.rem(r, 2) == s % 2)
        diag_only = jnp.logical_and(d_sender, jnp.logical_or(near_diag, far_diag))
        o_sender = jnp.logical_and(in_g, c != grp)
        dsem = in_recv_d.at[lax.rem(r, 2)]
        d_copy = rcopy(full_half, hb.at[0, rows], in_send.at[s], dsem, dev(q, s, grp))
        diag_copy = rcopy(ham.at[mat, :, diag_cols], hb.at[0, rows, diag_cols], in_send.at[s], dsem, dev(q, s, grp))
        o_copy = rcopy(full_half, hb.at[1, rows], in_send.at[s], in_recv_o.at[lax.rem(r, 2)], dev(q, s, g))
        def local():
            return pltpu.make_async_copy(full_half, hb.at[0, rows], dsem)
        return (own_d, local), ((far_full, d_copy), (diag_only, diag_copy), (o_sender, o_copy))

    for s in range(row_size):
        (own_d, local), copies = in_parts(s)
        pl.when(own_d)(lambda local=local: local().start())
        for cond, copy in copies:
            pl.when(cond)(copy.start)

    first_owner = r < slots
    my_slot = slot_of(r)
    alpha = c == grp
    mine = par * slots + my_slot
    peer = dev(q, r, 1 - c)
    final_d, final_o = (4, 5) if STEPS % 2 else (0, 1)

    def stat_exchange(k):
        return rcopy(ts.at[k], tr.at[k], t_send.at[k], t_recv.at[k], peer)

    def rowsum(x):
        return jnp.sum(x.reshape(x.shape[0] // 8, 8, x.shape[1]), axis=0)

    chunk = 128

    def chunks(body, init=None):
        return lax.fori_loop(0, order // chunk, lambda i, carry: body(aligned(i * chunk, chunk), i, carry), init)

    def total(v):
        return jnp.sum(jnp.sum(v, axis=1, keepdims=True), axis=0, keepdims=True)

    def tile(i):
        return aligned(i * half, half)

    def eye_of(i):
        ids = lax.broadcasted_iota(jnp.int32, (chunk, order), 0) + i * chunk
        return ids == lax.broadcasted_iota(jnp.int32, (chunk, order), 1)

    def diagonal(ref):
        ids = [lax.broadcasted_iota(jnp.int32, (chunk, chunk), k) for k in range(2)]
        acc = jnp.zeros((8, chunk), F32)
        for i in range(order // chunk):
            at = slice(i * chunk, (i + 1) * chunk)
            acc += rowsum(jnp.where(ids[0] == ids[1], ref[at, at], 0.0))
        return acc

    def rows_of(k):
        return pl.ds(k * piece, piece)

    def x_copy(which, dr, k):
        rr = lax.rem(r + dr, row_size)
        core = c if which == 0 else 1 - c
        start = lax.rem(rr, 2) * half + k * piece
        part = xb.at[final_o if which else final_d, aligned(start, piece)]
        sem = x_send.at[which, dr, k]
        arrived = x_recv.at[my_slot, k]
        if dr == 0 and which == 0:
            return pltpu.make_async_copy(part, out.at[mine, rows_of(k)], arrived)
        if dr != 2:
            return rcopy(part, out.at[mine, rows_of(k)], sem, arrived, dev(q, rr, core))
        via = lax.rem(r + (1 if k in up_pieces else row_size - 1), row_size)
        return rcopy(part, relay.at[k], sem, r_recv.at[k], dev(q, via, core))

    def sent_pieces(dr):
        shared = {0: in_turn, 1: up_pieces, 2: (), 3: down_pieces}[dr]
        return [(None if k in shared else alone(r), k) for k in in_turn]

    def guarded(cond, extra, action):
        pl.when(cond if extra is None else jnp.logical_and(cond, extra))(action)

    def x_starts(which, parity=None):
        for dr in (0, 2, 1, 3):
            rr = lax.rem(r + dr, row_size)
            cond = c == rr // 2
            if parity is not None:
                cond = jnp.logical_and(cond, lax.rem(rr, 2) == parity)
            for extra, k in sent_pieces(dr):
                guarded(cond, extra, lambda dr=dr, k=k: x_copy(which, dr, k).start())

    def p_copy(slot, t):
        i, j = t // 2, lax.rem(t, 2)
        return rcopy(ps.at[tile(i), tile(j)], pr.at[slot, tile(i), tile(j)], p_send.at[t], p_recv.at[slot, t], peer)

    def send_product(slot, lhs, rhs, before):
        def body(t, _):
            i, j = t // 2, lax.rem(t, 2)
            pl.when(before)(lambda: p_copy(1 - slot, t).wait_send())
            ps[tile(i), tile(j)] = dot_nn(xb[lhs, tile(i), :], xb[rhs, :, tile(j)])
            p_copy(slot, t).start()
            return 0
        lax.fori_loop(0, 4, body, 0)

    def purify():
        own_half = lax.rem(r, 2)
        whole = jnp.where(alpha, own_half, 1 - own_half)
        other = 1 - whole
        rows_w = aligned(whole * half, half)
        rows_o = aligned(other * half, half)

        def tmp_copy(k):
            rows = aligned(k * half, half)
            return rcopy(hb.at[1, rows], pr.at[1, rows], tmp_send.at[k], tmp_recv.at[k], peer)

        wait_for(hb.at[0, rows_o, rows_o], in_recv_d.at[other])
        wait_for(hb.at[0, rows_w], in_recv_d.at[whole])
        ts[0] = jnp.zeros(ts.shape[1:], F32)
        ts[0, 0, :, 0:chunk] = diagonal(hb.at[0])
        stat_exchange(0).start()
        hb[0, rows_o, rows_w] = hb[0, rows_w, rows_o].T

        @pl.when(alpha)
        def _():
            for k in (own_half, 1 - own_half):
                wait_for(hb.at[1, aligned(k * half, half)], in_recv_o.at[k])
                tmp_copy(k).start()

        @pl.when(jnp.logical_not(alpha))
        def _():
            for k in (own_half, 1 - own_half):
                tmp_copy(k).wait_recv()
                hb[1, :, aligned(k * half, half)] = pr[1, aligned(k * half, half), :].T

        @pl.when(alpha)
        def _():
            for k in range(2):
                tmp_copy(k).wait_send()

        stat_exchange(0).wait()
        n = float(full_order)
        mu = total(ts[0, 0] + tr[0, 0]) / n
        occupied = jnp.full((1, 1), occ[mine].astype(F32))
        eps_min = jnp.full((1, 1), bounds[0, mine])
        eps_max = jnp.full((1, 1), bounds[1, mine])
        lam = jnp.minimum(occupied / (eps_max - mu), (n - occupied) / (mu - eps_min))
        shift = (lam * mu + occupied) / n
        slope = lam / n

        def start_x(rows, i, _):
            xb[0, rows, :] = jnp.where(eye_of(i), shift, 0.0) - slope * hb[0, rows, :]
            xb[1, rows, :] = -(slope * hb[1, rows, :])
            return 0
        chunks(start_x, 0)

        def one_step(step, _):
            flip = lax.rem(step, 2)
            d_old, o_old = 4 * flip, 4 * flip + 1
            d_new, o_new = 4 - d_old, 6 - o_old
            k = 1 + step
            last = step == STEPS - 1

            ts[k] = jnp.zeros(ts.shape[1:], F32)
            ts[k, 0, :, 0:chunk] = diagonal(xb.at[d_old])
            send_product(0, d_old, o_old, step > 0)

            def join_sq(t):
                i, j = t // 2, lax.rem(t, 2)
                val = ps[tile(i), tile(j)] + pr[0, tile(j), tile(i)].T
                xb[3, tile(i), tile(j)] = val
                o = xb[o_old, tile(i), tile(j)]
                ts[k, 1] += rowsum(o * o)
                ts[k, 2] += rowsum(val * o)

            def sq_body(t, _):
                p_copy(0, lax.rem(t, 2) * 2 + t // 2).wait_recv()
                rows, cols = tile(t // 2), tile((t + 1) // 2)
                val = dot_nn(xb[d_old, rows, :], xb[d_old, :, cols]) + dot_nt(xb[o_old, rows, :], xb[o_old, cols, :])
                xb[2, rows, cols] = val
                d = xb[d_old, rows, cols]
                weight = jnp.where(t == 1, 2.0, 1.0)
                ts[k, 1] += weight * rowsum(d * d)
                ts[k, 2] += weight * rowsum(val * d)
                join_sq(t)

                @pl.when(t == 1)
                def _():
                    xb[2, half:order, 0:half] = xb[2, 0:half, half:order].T
                return 0
            lax.fori_loop(0, 3, sq_body, 0)
            p_copy(0, 3).wait_recv()
            join_sq(3)
            stat_exchange(k).start()

            send_product(1, jnp.where(c == 0, 2, d_old), jnp.where(c == 0, o_old, 3), True)
            stat_exchange(k).wait()
            t1, t2, t3 = (total(ts[k, i] + tr[k, i]) for i in range(3))
            coef = (t2 - t3) / (t1 - t2)
            inv = 1.0 / (1.0 - coef)
            ca, cb = (1.0 - 2.0 * coef) * inv, (1.0 + coef) * inv

            def join_new(t, _):
                i, j = t // 2, lax.rem(t, 2)
                p_copy(1, j * 2 + i).wait_recv()
                val = ps[tile(i), tile(j)] + pr[1, tile(j), tile(i)].T
                xb[o_new, tile(i), tile(j)] = ca * xb[o_old, tile(i), tile(j)] + cb * xb[3, tile(i), tile(j)] - inv * val
                return 0
            lax.fori_loop(0, 4, join_new, 0)
            pl.when(last)(lambda: x_starts(1))

            def cube_body(t, _):
                rows, cols = tile(t // 2), tile((t + 1) // 2)
                val = dot_nn(xb[2, rows, :], xb[d_old, :, cols]) + dot_nt(xb[3, rows, :], xb[o_old, cols, :])
                xb[d_new, rows, cols] = ca * xb[d_old, rows, cols] + cb * xb[2, rows, cols] - inv * val

                @pl.when(t == 1)
                def _():
                    xb[d_new, half:order, 0:half] = xb[d_new, 0:half, half:order].T
                for parity in range(2):
                    pl.when(jnp.logical_and(last, t == parity + 1))(lambda parity=parity: x_starts(0, parity))
                return 0
            lax.fori_loop(0, 3, cube_body, 0)
            return 0
        lax.fori_loop(0, STEPS, one_step, 0)
        for t in range(4):
            p_copy(1, t).wait_send()

    purify()

    def y_copy(s, k):
        part = out.at[par * slots + s, rows_of(k)]
        return rcopy(part, part, y_send.at[s, k], y_recv.at[s, k], dev(q_up if k in up_pieces else q_dn, r, c))

    def pass_on(cond, drs):
        for k in in_turn:
            for dr in drs:
                x = lax.rem(r + row_size - dr, row_size)
                shared = {0: in_turn, 1: up_pieces, 2: (), 3: down_pieces}[dr]

                def step_on(k=k, x=x):
                    at = slot_of(x)
                    wait_for(out.at[par * slots + at, rows_of(k)], x_recv.at[at, k])
                    y_copy(at, k).start()
                guarded(cond, None if k in shared else alone(x), step_on)

    r_up = lax.rem(r + 1, row_size)
    r_dn = lax.rem(r + row_size - 1, row_size)

    def relay_ends(k):
        return (r_dn, r_up) if k in up_pieces else (r_up, r_dn)

    def relay_copy(k):
        source, target = relay_ends(k)
        source = slot_of(source)
        return rcopy(relay.at[k], out.at[par * slots + source, rows_of(k)], r_send.at[k],
                     x_recv.at[source, k], dev(q, target, c))

    def relays(late):
        for k in in_turn:
            source, target = relay_ends(k)

            @pl.when(jnp.logical_and(alone(source), (c == target // 2) == late))
            def _(k=k):
                wait_for(relay.at[k], r_recv.at[k])
                relay_copy(k).start()

    early = c != grp
    pass_on(early, (0,))
    relays(False)
    pass_on(early, (1, 3))

    def e_copy(dr):
        return rcopy(es, er.at[mine], e_send.at[dr], e_recv.at[my_slot],
                     dev(q, lax.rem(r + dr, row_size), c))

    pass_on(jnp.logical_not(early), (0,))

    @pl.when(first_owner)
    def _():
        ts[STEPS + 1] = jnp.zeros(ts.shape[1:], F32)

        def energy_part(rows, i, _):
            v = rowsum(xb[final_d, rows, :] * hb[0, rows, :] + xb[final_o, rows, :] * hb[1, rows, :])
            ts[STEPS + 1, 0] += v[:, 0:half] + v[:, half:order]
            return 0
        chunks(energy_part, 0)
        stat_exchange(STEPS + 1).start()
        stat_exchange(STEPS + 1).wait()
        es[...] = jnp.broadcast_to(2.0 * total(ts[STEPS + 1, 0] + tr[STEPS + 1, 0]), es.shape)
        er[mine] = es[...]
        for dr in range(1, row_size):
            e_copy(dr).start()

    relays(True)
    pass_on(early, (2,))
    pass_on(jnp.logical_not(early), (1, 3))
    pass_on(jnp.logical_not(early), (2,))

    def ey_copy(s):
        tile_ref = er.at[par * slots + s]
        return rcopy(tile_ref, tile_ref, ey_send.at[s], ey_recv.at[s], dev(q_up, r, c))

    for s in range(slots):
        @pl.when(r != s)
        def _(s=s):
            wait_for(er.at[par * slots + s], e_recv.at[s])
        ey_copy(s).start()

    for s in range(slots):
        for k in range(PIECES):
            wait_for(out.at[(1 - par) * slots + s, rows_of(k)], y_recv.at[s, k])
            y_copy(s, k).wait_send()
        wait_for(er.at[(1 - par) * slots + s], ey_recv.at[s])
        ey_copy(s).wait_send()

    for k in range(PIECES):
        @pl.when(alone(relay_ends(k)[0]))
        def _(k=k):
            relay_copy(k).wait_send()
    for s in range(row_size):
        for cond, copy in in_parts(s)[1]:
            pl.when(cond)(copy.wait_send)

    for which in range(2):
        for dr in range(row_size):
            if which == 0 and dr == 0:
                continue
            for extra, k in sent_pieces(dr):
                guarded(c == lax.rem(r + dr, row_size) // 2, extra,
                        lambda which=which, dr=dr, k=k: x_copy(which, dr, k).wait_send())

    @pl.when(first_owner)
    def _():
        for dr in range(1, row_size):
            e_copy(dr).wait_send()

    energy_out[...] = er[...]


def solution(mesh):
    depth_size = mesh.shape['depth']
    row_size = mesh.shape['row']
    col_size = mesh.shape['col']

    def local_purify(ham_blk, spec_bounds, occ_count):
        kpoints, row_blk, col_blk = ham_blk.shape
        slots = kpoints // 2
        any_space = pl.BlockSpec(memory_space=pl.ANY)
        smem = pl.BlockSpec(memory_space=pltpu.SMEM)
        vmem = pl.BlockSpec(memory_space=pltpu.VMEM)
        dma = pltpu.SemaphoreType.DMA
        square = (col_blk, col_blk)
        density, energy, _ = pl.pallas_call(
            functools.partial(kernel, (slots, depth_size, row_size, col_size)),
            out_shape=(
                jax.ShapeDtypeStruct(ham_blk.shape, F32),
                jax.ShapeDtypeStruct((kpoints, 8, 128), F32),
                jax.ShapeDtypeStruct((PIECES, row_blk // PIECES, col_blk), F32),
            ),
            in_specs=[any_space, smem, smem],
            out_specs=(any_space, vmem, any_space),
            scratch_shapes=[
                pltpu.VMEM((2, *square), F32),
                pltpu.VMEM((6, *square), F32),
                pltpu.VMEM(square, F32),
                pltpu.VMEM((2, *square), F32),
                pltpu.VMEM((STEPS + 2, 3, 8, row_blk), F32),
                pltpu.VMEM((STEPS + 2, 3, 8, row_blk), F32),
                pltpu.VMEM((8, 128), F32),
                pltpu.VMEM((kpoints, 8, 128), F32),
                dma((row_size,)), dma((2,)), dma((2,)), dma((2,)), dma((2,)),
                dma((4,)), dma((2, 4)), dma((STEPS + 2,)), dma((STEPS + 2,)),
                dma((2, row_size, PIECES)), dma((slots, PIECES)), dma((PIECES,)), dma((PIECES,)),
                dma((slots, PIECES)), dma((slots, PIECES)), dma((row_size,)), dma((slots,)), dma((slots,)), dma((slots,)),
            ],
            compiler_params=pltpu.CompilerParams(
                collective_id=0, has_side_effects=True, vmem_limit_bytes=60 * 2**20
            ),
            name='purify',
        )(ham_blk, spec_bounds.T, occ_count)
        return density, energy[:, 0, 0]

    mat_spec = P('spin', 'row', 'col')
    return jax.shard_map(local_purify, mesh=mesh, in_specs=(mat_spec, P('spin', None), P('spin')), out_specs=(mat_spec, P('spin')), check_vma=False)
```

profile of v0, /device:TPU:96, one launch (start us, length us, event | category | flops | bytes accessed | tf_op | source)
XLA Modules:
  0.0 371.8 jit_solution(2406528386472986067)
XLA Ops:
  0.6 357.7 %purify.1 = (f32[6,512,1024]{2,1,0:T(8,128)}, f32[6,8,128]{2,1,0:T(8,128)}, f32[4,128,1024]{2,1,0:T(8,128)}) custom-call(f32[6,512,1024]{2,1,0:T(8,128)} %ham.1, f32[2,6]{1,0:T(2,128)} %bitcast.1, s32[6]{0:T(128)} %occ.1), custom_call_target="tpu_custom_call" | custom-call | tf_op jit(solution)/shard_map/purify/pallas_call | solution.py:437
  358.4 1.4 slice_reduce_fusion
  359.7 12.1 %copy.6 = f32[6,512,1024]{2,1,0:T(8,128)} copy(f32[6,512,1024]{2,1,0:T(8,128)} %get-tuple-element.8) | data formatting | bytes 25165824
where the time goes:
time: 375 us; the launch traced here: 372 us
  Pallas kernels  358 us (95%)
  local copies, waits for them, and re-layouts  13.5 us (4%)
    pallas_call x1, Pallas kernels, local_purify(): pl.pallas_call(functools.partial(kernel, (slots, depth_size, row_size, co...  358 us
    unnamed x1, local copies, waits for them, and re-layouts  12.1 us

commit v1 on v0

--- a/solution.py
+++ b/solution.py
@@ -300,6 +300,7 @@
                 @pl.when(t == 1)
                 def _():
                     xb[d_new, half:order, 0:half] = xb[d_new, 0:half, half:order].T
+                pl.when(jnp.logical_and(last, t == 0))(lambda: pass_on(early, (0,)))
                 for parity in range(2):
                     pl.when(jnp.logical_and(last, t == parity + 1))(lambda parity=parity: x_starts(0, parity))
                 return 0
@@ -309,8 +310,6 @@
         for t in range(4):
             p_copy(1, t).wait_send()
 
-    purify()
-
     def y_copy(s, k):
         part = out.at[par * slots + s, rows_of(k)]
         return rcopy(part, part, y_send.at[s, k], y_recv.at[s, k], dev(q_up if k in up_pieces else q_dn, r, c))
@@ -349,7 +348,7 @@
                 relay_copy(k).start()
 
     early = c != grp
-    pass_on(early, (0,))
+    purify()
     relays(False)
     pass_on(early, (1, 3))
 

time: 375 us -> 364 us (0.971)
  Pallas kernels: 358 us -> 347 us
    pallas_call x1, Pallas kernels: 358 us -> 347 us  [local_purify(): pl.pallas_call(functools.partial(kernel, (slots, depth_size, row_size, co...]
where the time goes in v1:
time: 364 us; the launch traced here: 361 us
  Pallas kernels  347 us (95%)
  local copies, waits for them, and re-layouts  13.5 us (4%)
    pallas_call x1, Pallas kernels, local_purify(): pl.pallas_call(functools.partial(kernel, (slots, depth_size, row_size, co...  347 us
    unnamed x1, local copies, waits for them, and re-layouts  12.1 us

profile of v1, /device:TPU:96, one launch (start us, length us, event | category | flops | bytes accessed | tf_op | source)
XLA Modules:
  0.0 360.8 jit_solution(18074785868419288569)
XLA Ops:
  0.6 346.7 %purify.1 = (f32[6,512,1024]{2,1,0:T(8,128)}, f32[6,8,128]{2,1,0:T(8,128)}, f32[4,128,1024]{2,1,0:T(8,128)}) custom-call(f32[6,512,1024]{2,1,0:T(8,128)} %ham.1, f32[2,6]{1,0:T(2,128)} %bitcast.1, s32[6]{0:T(128)} %occ.1), custom_call_target="tpu_custom_call" | custom-call | tf_op jit(solution)/shard_map/purify/pallas_call | solution.py:436
  347.3 1.4 slice_reduce_fusion
  348.7 12.1 %copy.6 = f32[6,512,1024]{2,1,0:T(8,128)} copy(f32[6,512,1024]{2,1,0:T(8,128)} %get-tuple-element.8) | data formatting | bytes 25165824
